TPU v7x, 32 devices: a whole 2x2x4 slice. The times are simulated.
32 devices in a mesh: row: 4 (over z), col: 8 (over y, x, core).
Axes of the slice: x: 2, y: 2, z: 4, core: 2. Of those that a mesh axis runs over, the one named last changes fastest.
Arguments:
- coefs: float32 [2, 384, 16384], P(None, 'row', 'col'), may hold values from -600 to 600, as said below
- tilts: int32 [384, 2], replicated, may hold values from 8 to 48
- start_basis: float32 [384, 32], P('col'), may hold values from -6 to 6
Outputs:
- ccc: float32 [384, 384], P('row', 'col')
- basis: float32 [384, 32], P('col')
Inputs may be any that keep to these rules, and one draw needn't show every extreme that they name: `coefs`: real and imaginary parts are products of a particle scale, a coefficient scale and a bounded random value.
All inputs are finite; a program needn't handle non-finite values.
Results may differ from a plain program's by a relative error of at most 0.0003.
Values sent between devices are 32-bit elements; how exact they have to be, the bound alone decides.
A program may use at most 192 MiB of HBM per device.

v0:
```python
import math

import jax
import jax.numpy as jnp
from jax import lax
from jax.sharding import PartitionSpec as P

GRID = 32
ITERS = 4


EPS = 1e-06
HIGH = lax.Precision.HIGHEST


def wedge(tilt_rows, wave_index):
    wave_x = jnp.abs(wave_index // (GRID * (GRID // 2)) - GRID // 2)[None, :]
    wave_z = (wave_index % GRID - GRID // 2)[None, :]
    upward = wave_z * 16 <= tilt_rows[:, 1:2] * wave_x
    downward = -wave_z * 16 <= tilt_rows[:, 0:1] * wave_x
    return jnp.where(wave_z >= 0, upward, downward).astype(jnp.float32)


def inner(left, right):
    return lax.dot_general(
        left, right, (((1,), (1,)), ((), ())), precision=HIGH, preferred_element_type=jnp.float32
    )


def prepare(values, tilt_rows, wave_index):
    masks = wedge(tilt_rows, wave_index)
    paired = jnp.concatenate([values[0] * masks, values[1] * masks], axis=1)
    energy = masks * (values[0] * values[0] + values[1] * values[1])
    return (masks, paired, energy)


def local(coefs, tilts, start_basis):
    row_count = coefs.shape[1]
    slice_width = coefs.shape[2]
    col_count = start_basis.shape[0]
    col_size = lax.axis_size("col")
    total = col_count * col_size
    row_index = lax.axis_index("row")
    col_index = lax.axis_index("col")
    own_tilts = lax.dynamic_slice_in_dim(tilts, row_index * row_count, row_count, 0)
    wave_index = col_index * slice_width + jnp.arange(slice_width, dtype=jnp.int32)
    own_mask, own_pair, own_energy = prepare(coefs, own_tilts, wave_index)
    gathered = lax.all_gather(coefs, "row", axis=1, tiled=True)
    mask_j, pair_j, energy_j = prepare(gathered, tilts, wave_index)
    numer = inner(pair_j, own_pair)
    first = inner(mask_j, own_energy)
    second = inner(energy_j, own_mask)
    summed = lax.psum_scatter(
        jnp.concatenate([numer, first, second], axis=1), "col", scatter_dimension=0, tiled=True
    )
    numer = summed[:, :row_count]
    first = summed[:, row_count : 2 * row_count]
    second = summed[:, 2 * row_count :]
    block = (numer / jnp.sqrt(first * second + EPS)).T
    current = start_basis
    for step in range(ITERS):
        partial_value = jnp.dot(block, current, precision=HIGH, preferred_element_type=jnp.float32)
        summed_rows = lax.psum(partial_value, "col")
        local_gram = lax.dot_general(
            summed_rows,
            summed_rows,
            (((0,), (0,)), ((), ())),
            precision=HIGH,
            preferred_element_type=jnp.float32,
        )
        gram = lax.psum(local_gram, "row")
        factor = jnp.linalg.cholesky(gram)
        fresh = lax.linalg.triangular_solve(
            factor, summed_rows, left_side=False, lower=True, transpose_a=True
        )
        whole = lax.all_gather(fresh, "row", axis=0, tiled=True)
        current = lax.dynamic_slice_in_dim(whole, col_index * col_count, col_count, 0)
    return (block, current * math.sqrt(total))


def solution(mesh):
    in_specs = (P(None, "row", "col"), P(), P("col", None))
    out_specs = (P("row", "col"), P("col", None))
    return jax.shard_map(local, mesh=mesh, in_specs=in_specs, out_specs=out_specs, check_vma=False)
```

profile of v0, /device:TPU:0, one launch (start us, length us, event | category | flops | bytes accessed | tf_op | source)
XLA Modules:
  0.0 422.8 jit_solution(8679208534305008273)
XLA Ops:
  8.0 0.8 constant_dynamic-slice_fusion
  8.8 0.8 slice_reduce_fusion.1
  9.6 4.0 fusion.18
  14.0 113.6 %all-gather.6.cloned.1.call-done = f32[2,384,2048]{2,1,0:T(8,128)} async-done(((f32[2,96,2048]{2,1,0:T(8,128)}), f32[2,384,2048]{2,1,0:T(8,128)}) %all-gather.6.cloned.1.call-update) | async-done | bytes 6291472 | tf_op jit(solution)/shard_map/all_gather | solution.py:48
  127.6 4.1 fusion.10
  131.8 6.0 %fusion = f32[384,96]{0,1:T(8,128)S(1)} fusion(f32[384,2048]{1,0:T(8,128)S(1)} %get-tuple-element.13, f32[384,2048]{1,0:T(8,128)S(1)} %get-tuple-element.12, f32[96,2048]{1,0:T(8,128)S(1)} %get-tuple-element.15, f32[96,2048]{1,0:T(8,128)S(1)} %get-tuple-element.14), kind=kOutput, calls=%fused_computation | convolution fusion | flops 1813905408 | bytes 8011776 | tf_op jit(solution)/shard_map/dot_general | solution.py:25
  137.8 3.2 fusion.4
  141.1 1.2 copy.44
  142.3 32.7 %reduce-scatter.4.cloned.1.call-done = f32[48,288]{1,0:T(8,128)} async-done(((f32[384,288]{1,0:T(8,128)}), f32[48,288]{1,0:T(8,128)}) %reduce-scatter.4.cloned.1.call-update) | async-done | bytes 55312
  175.0 0.9 fusion.67
  176.5 22.5 %psum.56 = f32[96,32]{0,1:T(8,128)S(1)} all-reduce(f32[96,32]{0,1:T(8,128)S(1)} %fusion.68), channel_id=1, replica_groups=mesh['row'=4,'col'=8] {'col'}, use_global_device_ids=true, to_apply=%region_1.2 | all-reduce | flops 3072 | bytes 24576 | tf_op jit(solution)/shard_map/psum | solution.py:63
  199.2 18.7 %psum.57 = f32[32,32]{0,1:T(8,128)S(1)} all-reduce(f32[32,32]{0,1:T(8,128)S(1)} %fusion.69), channel_id=1, replica_groups=mesh['row'=4,'col'=8] {'row'}, use_global_device_ids=true, to_apply=%region_2.3 | all-reduce | flops 1024 | bytes 8192 | tf_op jit(solution)/shard_map/psum | solution.py:71
  218.0 2.9 cholesky.74
  222.2 2.4 custom-call.8
  224.9 0.7 copy.39
  225.6 13.1 %all-gather = f32[4,96,32]{1,2,0:T(8,128)S(1)} all-gather(f32[1,96,32]{1,2,0:T(8,128)S(1)} %convolution_bitcast_fusion.3), channel_id=1, replica_groups=mesh['row'=4,'col'=8] {'row'}, dimensions={0}, use_global_device_ids=true | all-gather | bytes 61440 | tf_op jit(solution)/shard_map/all_gather | solution.py:76
  239.1 22.3 %psum.58 = f32[96,32]{0,1:T(8,128)S(1)} all-reduce(f32[96,32]{0,1:T(8,128)S(1)} %fusion.46), channel_id=1, replica_groups=mesh['row'=4,'col'=8] {'col'}, use_global_device_ids=true, to_apply=%region_5.8 | all-reduce | flops 3072 | bytes 24576 | tf_op jit(solution)/shard_map/psum | solution.py:63
  261.5 15.5 %psum.59 = f32[32,32]{0,1:T(8,128)S(1)} all-reduce(f32[32,32]{0,1:T(8,128)S(1)} %fusion.70), channel_id=1, replica_groups=mesh['row'=4,'col'=8] {'row'}, use_global_device_ids=true, to_apply=%region_6.9 | all-reduce | flops 1024 | bytes 8192 | tf_op jit(solution)/shard_map/psum | solution.py:71
  277.2 2.9 cholesky.85
  281.4 2.4 custom-call.9
  284.1 13.1 %all-gather.1 = f32[4,96,32]{1,2,0:T(8,128)S(1)} all-gather(f32[1,96,32]{1,2,0:T(8,128)S(1)} %convolution_bitcast_fusion.2), channel_id=1, replica_groups=mesh['row'=4,'col'=8] {'row'}, dimensions={0}, use_global_device_ids=true | all-gather | bytes 61440 | tf_op jit(solution)/shard_map/all_gather | solution.py:76
  297.6 22.3 %psum.60 = f32[96,32]{0,1:T(8,128)S(1)} all-reduce(f32[96,32]{0,1:T(8,128)S(1)} %fusion.44), channel_id=1, replica_groups=mesh['row'=4,'col'=8] {'col'}, use_global_device_ids=true, to_apply=%region_7.10 | all-reduce | flops 3072 | bytes 24576 | tf_op jit(solution)/shard_map/psum | solution.py:63
  320.1 16.3 %psum.61 = f32[32,32]{0,1:T(8,128)S(1)} all-reduce(f32[32,32]{0,1:T(8,128)S(1)} %fusion.71), channel_id=1, replica_groups=mesh['row'=4,'col'=8] {'row'}, use_global_device_ids=true, to_apply=%region_8.11 | all-reduce | flops 1024 | bytes 8192 | tf_op jit(solution)/shard_map/psum | solution.py:71
  336.5 2.9 cholesky.96
  340.7 2.4 custom-call.10
  343.4 13.1 %all-gather.2 = f32[4,96,32]{1,2,0:T(8,128)S(1)} all-gather(f32[1,96,32]{1,2,0:T(8,128)S(1)} %convolution_bitcast_fusion.1), channel_id=1, replica_groups=mesh['row'=4,'col'=8] {'row'}, dimensions={0}, use_global_device_ids=true | all-gather | bytes 61440 | tf_op jit(solution)/shard_map/all_gather | solution.py:76
  356.9 22.3 %psum.62 = f32[96,32]{0,1:T(8,128)S(1)} all-reduce(f32[96,32]{0,1:T(8,128)S(1)} %fusion.42), channel_id=1, replica_groups=mesh['row'=4,'col'=8] {'col'}, use_global_device_ids=true, to_apply=%region_9.12 | all-reduce | flops 3072 | bytes 24576 | tf_op jit(solution)/shard_map/psum | solution.py:63
  379.4 15.5 %psum.63 = f32[32,32]{0,1:T(8,128)S(1)} all-reduce(f32[32,32]{0,1:T(8,128)S(1)} %fusion.72), channel_id=1, replica_groups=mesh['row'=4,'col'=8] {'row'}, use_global_device_ids=true, to_apply=%region_10.13 | all-reduce | flops 1024 | bytes 8192 | tf_op jit(solution)/shard_map/psum | solution.py:71
  395.0 2.9 cholesky.107
  399.3 2.4 custom-call.11
  402.0 13.1 %all-gather.3 = f32[4,96,32]{1,2,0:T(8,128)S(1)} all-gather(f32[1,96,32]{1,2,0:T(8,128)S(1)} %convolution_bitcast_fusion), channel_id=1, replica_groups=mesh['row'=4,'col'=8] {'row'}, dimensions={0}, use_global_device_ids=true | all-gather | bytes 61440 | tf_op jit(solution)/shard_map/all_gather | solution.py:76
  415.2 0.7 dynamic-slice_multiply_fusion
  (60 shorter events, 10.1 us)
Async XLA Ops:
  7.2 169.1 %copy-start = (f32[48,32]{0,1:T(8,128)S(1)}, f32[48,32]{0,1:T(8,128)}, u32[]{:S(2)}) copy-start(f32[48,32]{0,1:T(8,128)} %param.8) | copy-start | bytes 18436
  7.2 120.5 %all-gather.6.cloned.1.call-start = ((), (), s32[]{:S(2)}) async-start(), calls=%async_computation.1 | async-start | bytes 7864320 | tf_op jit(solution)/shard_map/all_gather | solution.py:48
  7.9 167.1 %reduce-scatter.4.cloned.1.call-start = ((), (), s32[]{:S(2)}) async-start(), calls=%async_computation.2 | async-start | bytes 663552
  9.6 4.0 copy-start.1
  131.8 6.0 %copy-start.2 = (f32[2,384,2048]{2,1,0:T(8,128)S(1)}, f32[2,384,2048]{2,1,0:T(8,128)}, u32[]{:S(2)}) copy-start(f32[2,384,2048]{2,1,0:T(8,128)} %all-gather.6.cloned.1.call-done) | copy-start | bytes 18874372
Sparse Core Ops, SparseCore 0:
  9.6 118.0 all-gather.5
  142.5 32.5 reduce-scatter.3
where the time goes:
time: 423 us
  blocking collectives  208 us (49%)
  waiting for transfers between devices  147 us (35%)
  other arithmetic  32.1 us (8%)
  matrix products  15.6 us (4%)
  between operations  14.4 us (3%)
  local copies, waits for them, and re-layouts  5.54 us (1%)
    all_gather x1, waiting for transfers between devices, local(): gathered = lax.all_gather(coefs, 'row', axis=1, tiled=True)  114 us
    psum x4, blocking collectives, local(): summed_rows = lax.psum(partial_value, 'col')  89.5 us
    psum x4, blocking collectives, local(): gram = lax.psum(local_gram, 'row')  66.1 us
    all_gather x4, blocking collectives, local(): whole = lax.all_gather(fresh, 'row', axis=0, tiled=True)  52.5 us
    unnamed x3, waiting for transfers between devices  33.4 us
    another operation x12, other arithmetic, local(): factor = jnp.linalg.cholesky(gram)  14.4 us
    dot_general x3, matrix products, inner(): lax.dot_general(left, right, (((1,), (1,)), ((), ())), precision=HIGH, pr...  13.2 us
    another operation x8, other arithmetic, local(): lax.linalg.triangular_solve(factor, summed_rows, left_side=False, lower=T...  12.3 us
  transfers between devices with their start and end apart: 2, of which 2 were waited for; matrix products, arithmetic and copies ran while one was open for 1% of the time, Pallas kernels for 0%

commit v1 on v0

v1 whole, which is shorter than its diff:
```python
import functools
import math

import jax
import jax.numpy as jnp
from jax import lax
from jax.experimental import pallas as pl
from jax.experimental.pallas import tpu as pltpu
from jax.sharding import PartitionSpec as P

GRID = 32
ITERS = 4
EPS = 1e-06
HIGH = lax.Precision.HIGHEST
MESH = pl.DeviceIdType.MESH
TILE = 128
BLOCKS = 3


def flip(index, mask):
    out = index
    bit = 1
    while bit <= mask:
        if mask & bit:
            out = out + bit * (1 - 2 * ((index // bit) % 2))
        bit *= 2
    return out


def far_first(count):
    return sorted(range(1, count), key=lambda mask: (-mask.bit_length(), mask))


def split(value):
    high = value.astype(jnp.bfloat16)
    low = (value - high.astype(jnp.float32)).astype(jnp.bfloat16)
    return high, low


def thirds(value):
    high = value.astype(jnp.bfloat16)
    rest = value - high.astype(jnp.float32)
    middle, low = split(rest)
    return high, middle, low


def nt(left, right, precision=None):
    return lax.dot_general(
        left, right, (((1,), (1,)), ((), ())), precision=precision, preferred_element_type=jnp.float32
    )


def nn(left, right, precision=None):
    return lax.dot_general(
        left, right, (((1,), (0,)), ((), ())), precision=precision, preferred_element_type=jnp.float32
    )


def nn_six(left, right):
    lh, lm, ll = thirds(left)
    rh, rm, rl = thirds(right)
    small = nn(lm, rm) + nn(lh, rl) + nn(ll, rh)
    return nn(lh, rh) + (nn(lh, rm) + nn(lm, rh) + small)


def inverse_factor(gram):
    n = gram.shape[0]
    rows = lax.broadcasted_iota(jnp.int32, (n, n), 0)
    cols = lax.broadcasted_iota(jnp.int32, (n, n), 1)
    work = gram
    inverse = jnp.where(rows == cols, 1.0, 0.0).astype(jnp.float32)
    pivots = jnp.ones((n, n), jnp.float32)
    for j in range(n):
        column = jnp.broadcast_to(work[:, j : j + 1], (n, n))
        pivot = column[j : j + 1, :]
        reciprocal = 1.0 / pivot
        pivots = jnp.where(rows == j, pivot, pivots)
        factor = jnp.where(rows > j, column, 0.0)
        inverse = inverse - factor * (inverse[j : j + 1, :] * reciprocal)
        if j < n - 1:
            work = work - factor * (work[j : j + 1, :] * reciprocal)
    return inverse / jnp.sqrt(pivots)


def kernel(
    row_size, col_size, coefs_ref, tilts_ref, basis_ref, ccc_ref, out_ref,
    xall, start, xh, xl, eh, el, mb, part, rx_pair, rx_plane, rx_row, packed, ch, cl,
    own_sem, x_send, x_recv, v_send, v_recv, pair_send, pair_recv, plane_send, plane_recv,
    row_send, row_recv, zg_send, zg_recv, cg_send, cg_recv,
):
    z = lax.axis_index("row")
    c = lax.axis_index("col")
    rows = coefs_ref.shape[1]
    width = coefs_ref.shape[2]
    total = rows * row_size
    piece = width // row_size
    basis_rows = basis_ref.shape[0]
    size = total // BLOCKS

    barrier = pltpu.get_barrier_semaphore()
    for mask in range(1, row_size):
        pl.semaphore_signal(barrier, inc=1, device_id={"row": flip(z, mask)}, device_id_type=MESH)
    for mask in range(1, col_size):
        pl.semaphore_signal(barrier, inc=1, device_id={"col": flip(c, mask)}, device_id_type=MESH)
    pl.semaphore_wait(barrier, row_size + col_size - 2)

    def remote(source, target, send, recv, mask, axis):
        other = flip(z if axis == "row" else c, mask)
        return pltpu.make_async_remote_copy(
            src_ref=source, dst_ref=target, send_sem=send.at[mask - 1], recv_sem=recv.at[mask - 1],
            device_id={axis: other}, device_id_type=MESH,
        )

    own_rows = pl.ds(pl.multiple_of(z * rows, 8), rows)
    exchange = {}
    for mask in far_first(row_size):
        lanes = pl.ds(pl.multiple_of(flip(z, mask) * piece, TILE), piece)
        exchange[mask] = remote(coefs_ref.at[:, :, lanes], xall.at[:, own_rows, :], x_send, x_recv, mask, "row")
        exchange[mask].start()
    own = pltpu.make_async_copy(
        coefs_ref.at[:, :, pl.ds(pl.multiple_of(z * piece, TILE), piece)], xall.at[:, own_rows, :], own_sem
    )
    own.start()
    start_rows = pl.ds(pl.multiple_of(c * basis_rows, 8), basis_rows)
    start[start_rows, :] = basis_ref[...]
    starts = []
    for mask in range(1, col_size):
        copy = remote(basis_ref, start.at[start_rows, :], v_send, v_recv, mask, "col")
        copy.start()
        starts.append(copy)

    wave = c * width + z * piece + lax.broadcasted_iota(jnp.int32, (1, piece), 1)
    wave_x = jnp.abs(wave // (GRID * (GRID // 2)) - GRID // 2)
    wave_z = wave % GRID - GRID // 2

    def prepare(index):
        span = pl.ds(pl.multiple_of(index * rows, 16), rows)
        tilt = tilts_ref[span, :]
        upward = wave_z * 16 <= tilt[:, 1:2] * wave_x
        downward = -wave_z * 16 <= tilt[:, 0:1] * wave_x
        mask = jnp.where(jnp.logical_or(jnp.logical_and(wave_z >= 0, upward), jnp.logical_and(wave_z < 0, downward)), 1.0, 0.0)
        mb[span, :] = mask.astype(jnp.bfloat16)
        real = xall[0, span, :] * mask
        imag = xall[1, span, :] * mask
        xh[span, :piece], xl[span, :piece] = split(real)
        xh[span, piece:], xl[span, piece:] = split(imag)
        eh[span, :], el[span, :] = split(real * real + imag * imag)

    own.wait()
    prepare(z)
    for mask in reversed(far_first(row_size)):
        exchange[mask].wait()
        prepare(flip(z, mask))

    for a in range(BLOCKS):
        for t in range(2):
            b = (a + t) % BLOCKS
            right = slice(b * size, (b + 1) * size)
            lanes = slice(t * size, (t + 1) * size)

            def tile(index, carry, a=a, right=right, lanes=lanes):
                left = pl.ds(pl.multiple_of(a * size + index * TILE, TILE), TILE)
                part[0, left, lanes] = (
                    nt(xh[left, :], xh[right, :]) + nt(xh[left, :], xl[right, :]) + nt(xl[left, :], xh[right, :])
                )
                part[1, left, lanes] = nt(eh[left, :], mb[right, :]) + nt(el[left, :], mb[right, :])
                part[2, left, lanes] = nt(mb[left, :], eh[right, :]) + nt(mb[left, :], el[right, :])
                return carry

            lax.fori_loop(0, size // TILE, tile, 0)

    pairs = col_size // 2
    side = c % 2
    half = total // 2
    strip = total // col_size
    theirs = pl.ds(pl.multiple_of((1 - side) * half, 8), half)
    mine = pl.ds(pl.multiple_of(side * half, 8), half)
    pair = remote(part.at[:, theirs, :], rx_pair, pair_send, pair_recv, 1, "col")
    pair.start()
    pair.wait()
    part[:, mine, :] = part[:, mine, :] + rx_pair[...]
    group = c // 2
    copies = []
    for mask in far_first(pairs):
        there = pl.ds(pl.multiple_of(side * half + flip(group, mask) * strip, 8), strip)
        copy = pltpu.make_async_remote_copy(
            src_ref=part.at[:, there, :], dst_ref=rx_plane.at[mask - 1],
            send_sem=plane_send.at[mask - 1], recv_sem=plane_recv.at[mask - 1],
            device_id={"col": flip(c, 2 * mask)}, device_id_type=MESH,
        )
        copy.start()
        copies.append(copy)
    for copy in copies:
        copy.wait()
    base = side * half + group * strip
    strip_rows = pl.ds(pl.multiple_of(base, 8), strip)
    part[:, strip_rows, :] = part[:, strip_rows, :] + sum(rx_plane[k] for k in range(pairs - 1))

    cuts = row_size // 2
    short = strip // cuts

    def region(index):
        return (
            pl.ds(pl.multiple_of(base + (index // 2) * short, 8), short),
            pl.ds(pl.multiple_of((index % 2) * size, TILE), size),
        )

    copies = []
    for mask in far_first(row_size):
        there = region(flip(z, mask))
        copy = remote(part.at[:, there[0], there[1]], rx_row.at[mask - 1], row_send, row_recv, mask, "row")
        copy.start()
        copies.append(copy)
    for copy in copies:
        copy.wait()
    here = region(z)
    sums = part[:, here[0], here[1]] + sum(rx_row[k] for k in range(row_size - 1))
    packed[here[0], here[1]] = sums[0] / jnp.sqrt(sums[1] * sums[2] + EPS)

    copies = []
    for mask in far_first(row_size):
        spot = packed.at[here[0], here[1]]
        copy = remote(spot, spot, zg_send, zg_recv, mask, "row")
        copy.start()
        copies.append(copy)
    for copy in copies:
        copy.wait()
    copies = []
    for mask in far_first(col_size):
        spot = packed.at[strip_rows, :]
        copy = remote(spot, spot, cg_send, cg_recv, mask, "col")
        copy.start()
        copies.append(copy)
    for copy in copies:
        copy.wait()

    def place(i, j, value):
        down, across = slice(i, i + TILE), slice(j, j + TILE)
        plane, lane = (0, j) if j < 2 * size else (1, j - 2 * size)
        part[plane, down, lane : lane + TILE] = value
        ch[down, across], cl[down, across] = split(value)

    for a in range(BLOCKS):
        for t in range(2):
            b = (a + t) % BLOCKS
            for i in range(0, size, TILE):
                for j in range(0, size, TILE):
                    block = packed[a * size + i : a * size + i + TILE, t * size + j : t * size + j + TILE]
                    place(a * size + i, b * size + j, block)
                    if t:
                        place(b * size + j, a * size + i, block.T)

    chosen = lax.broadcasted_iota(jnp.int32, (basis_rows, total), 1)
    chosen = chosen == c * basis_rows + lax.broadcasted_iota(jnp.int32, (basis_rows, total), 0)
    chosen = jnp.where(chosen, 1.0, 0.0).astype(jnp.float32)
    ccc_ref[...] = nt(part[0, own_rows, :], chosen[:, : 2 * size], HIGH) + nt(
        part[1, own_rows, :size], chosen[:, 2 * size :], HIGH
    )

    for copy in starts:
        copy.wait()
    eig = basis_ref.shape[1]
    unit = lax.broadcasted_iota(jnp.int32, (eig, eig), 0) == lax.broadcasted_iota(jnp.int32, (eig, eig), 1)
    first = nt(jnp.where(unit, 1.0, 0.0).astype(jnp.float32), start[...], HIGH)

    def iterate(step, current):
        high, low = split(current)
        wide = nn(high, ch[...]) + nn(high, cl[...]) + nn(low, ch[...])
        return nn_six(inverse_factor(nt(wide, wide, HIGH)), wide)

    last = first
    for step in range(ITERS):
        last = iterate(step, last)
    out_ref[...] = nt(chosen, last, HIGH) * math.sqrt(total)


def local(coefs, tilts, start_basis):
    row_size = lax.axis_size("row")
    col_size = lax.axis_size("col")
    rows, width = coefs.shape[1:]
    basis_rows, eig = start_basis.shape
    total = rows * row_size
    piece = width // row_size
    lanes = 2 * (total // BLOCKS)
    strip = total // col_size
    pairs = col_size // 2
    f32, b16 = jnp.float32, jnp.bfloat16
    dma = lambda n: pltpu.SemaphoreType.DMA((n,))
    vmem = pl.BlockSpec(memory_space=pltpu.VMEM)
    ccc, basis = pl.pallas_call(
        functools.partial(kernel, row_size, col_size),
        out_shape=(
            jax.ShapeDtypeStruct((rows, basis_rows), f32),
            jax.ShapeDtypeStruct((basis_rows, eig), f32),
        ),
        in_specs=[pl.BlockSpec(memory_space=pl.ANY), vmem, vmem],
        out_specs=(vmem, vmem),
        scratch_shapes=[
            pltpu.VMEM((2, total, piece), f32),
            pltpu.VMEM((total, eig), f32),
            pltpu.VMEM((total, 2 * piece), b16),
            pltpu.VMEM((total, 2 * piece), b16),
            pltpu.VMEM((total, piece), b16),
            pltpu.VMEM((total, piece), b16),
            pltpu.VMEM((total, piece), b16),
            pltpu.VMEM((3, total, lanes), f32),
            pltpu.VMEM((3, total // 2, lanes), f32),
            pltpu.VMEM((pairs - 1, 3, strip, lanes), f32),
            pltpu.VMEM((row_size - 1, 3, strip // (row_size // 2), lanes // 2), f32),
            pltpu.VMEM((total, lanes), f32),
            pltpu.VMEM((total, total), b16),
            pltpu.VMEM((total, total), b16),
            pltpu.SemaphoreType.DMA,
            dma(row_size - 1), dma(row_size - 1),
            dma(col_size - 1), dma(col_size - 1),
            dma(1), dma(1),
            dma(pairs - 1), dma(pairs - 1),
            dma(row_size - 1), dma(row_size - 1),
            dma(row_size - 1), dma(row_size - 1),
            dma(col_size - 1), dma(col_size - 1),
        ],
        compiler_params=pltpu.CompilerParams(
            collective_id=0, has_side_effects=True, vmem_limit_bytes=67043328
        ),
        name="subspace",
    )(coefs, tilts, start_basis)
    return ccc, basis


def solution(mesh):
    in_specs = (P(None, "row", "col"), P(), P("col", None))
    out_specs = (P("row", "col"), P("col", None))
    return jax.shard_map(local, mesh=mesh, in_specs=in_specs, out_specs=out_specs, check_vma=False)
```

time: 423 us -> 88 us (0.21)
  blocking collectives: 208 us -> 0 us
  waiting for transfers between devices: 147 us -> 0 us
  Pallas kernels: 0 us -> 81.2 us
  other arithmetic: 32.1 us -> 0 us
  matrix products: 15.6 us -> 0 us
  between operations: 14.4 us -> 0.64 us
    psum x8 -> x0, blocking collectives: 156 us -> none  [the longest x4 89.5 us: local(): summed_rows = lax.psum(partial_value, 'col')]
    all_gather x1 -> x0, waiting for transfers between devices: 114 us -> none  [local(): gathered = lax.all_gather(coefs, 'row', axis=1, tiled=True)]
    pallas_call x0 -> x1, Pallas kernels: none -> 81.2 us  [local(): pl.pallas_call(functools.partial(kernel, row_size, col_size), out_shape=(...]
    all_gather x4 -> x0, blocking collectives: 52.5 us -> none  [local(): whole = lax.all_gather(fresh, 'row', axis=0, tiled=True)]
    unnamed x3 -> x0, waiting for transfers between devices: 33.4 us -> none
    another operation x20 -> x0, other arithmetic: 26.7 us -> none  [the longest x12 14.4 us: local(): factor = jnp.linalg.cholesky(gram)]
    dot_general x11 -> x0, matrix products: 14.7 us -> none  [the longest x3 13.2 us: inner(): lax.dot_general(left, right, (((1,), (1,)), ((), ())), precision=HIGH, pr...]
    mul x4 -> x0, other arithmetic: 5.26 us -> none  [the longest x2 4.56 us: prepare(): paired = jnp.concatenate([values[0] * masks, values[1] * masks], axis=1)]
  transfers between devices with their start and end apart: 2 -> 0, of which waited for: 2 -> 0; matrix products, arithmetic and copies ran while one was open for 1% -> 0% of each run, Pallas kernels for 0% -> 0%
where the time goes in v1:
time: 88 us; the launch traced here: 87.6 us
  Pallas kernels  81.2 us (92%)
  local copies, waits for them, and re-layouts  5.8 us (7%)
    pallas_call x1, Pallas kernels, local(): pl.pallas_call(functools.partial(kernel, row_size, col_size), out_shape=(...  81.2 us
    unnamed x2, local copies, waits for them, and re-layouts  2.9 us
    pallas_call x2, local copies, waits for them, and re-layouts, local(): pl.pallas_call(functools.partial(kernel, row_size, col_size), out_shape=(...  2.9 us

profile of v1, /device:TPU:0, one launch (start us, length us, event | category | flops | bytes accessed | tf_op | source)
XLA Modules:
  0.0 87.6 jit_solution(15212073195985506570)
XLA Ops:
  0.6 1.4 %copy.6.basis_ref = f32[48,32]{1,0:T(8,128)} copy(f32[48,32]{0,1:T(8,128)} %param.5) | data formatting | bytes 12288 | tf_op args[2]
  2.0 1.5 %copy.5.tilts_ref = s32[384,2]{1,0:T(8,128)} copy(s32[384,2]{0,1:T(2,128)} %param.4) | data formatting | bytes 6144 | tf_op args[1]
  3.5 81.2 %subspace.1 = (f32[96,48]{1,0:T(8,128)}, f32[48,32]{1,0:T(8,128)}) custom-call(f32[2,96,2048]{2,1,0:T(8,128)} %coefs_ref.1, s32[384,2]{1,0:T(8,128)} %copy.5.tilts_ref, f32[48,32]{1,0:T(8,128)} %copy.6.basis_ref), custom_call_target="tpu_custom_call" | custom-call | tf_op jit(solution)/shard_map/subspace/pallas_call | solution.py:290
  84.7 1.5 %copy.7 = f32[96,48]{0,1:T(8,128)} copy(f32[96,48]{1,0:T(8,128)} %get-tuple-element.2) | data formatting | bytes 36864 | tf_op jit(solution)/shard_map/subspace/pallas_call | solution.py:290
  86.2 1.4 %copy.8 = f32[48,32]{0,1:T(8,128)} copy(f32[48,32]{1,0:T(8,128)} %get-tuple-element.3) | data formatting | bytes 12288 | tf_op jit(solution)/shard_map/subspace/pallas_call | solution.py:290

commit v2 on v1

--- a/solution.py
+++ b/solution.py
@@ -84,7 +84,7 @@
 
 def kernel(
     row_size, col_size, coefs_ref, tilts_ref, basis_ref, ccc_ref, out_ref,
-    xall, start, xh, xl, eh, el, mb, part, rx_pair, rx_plane, rx_row, packed, ch, cl,
+    xall, start, first, keep, energy, xh, xl, eh, el, mb, part, rx_pair, rx_plane, rx_row, packed, ch, cl,
     own_sem, x_send, x_recv, v_send, v_recv, pair_send, pair_recv, plane_send, plane_recv,
     row_send, row_recv, zg_send, zg_recv, cg_send, cg_recv,
 ):
@@ -94,7 +94,8 @@
     width = coefs_ref.shape[2]
     total = rows * row_size
     piece = width // row_size
-    basis_rows = basis_ref.shape[0]
+    eig, basis_rows = basis_ref.shape
+    chunks = piece // TILE
     size = total // BLOCKS
 
     barrier = pltpu.get_barrier_semaphore()
@@ -113,61 +114,95 @@
 
     own_rows = pl.ds(pl.multiple_of(z * rows, 8), rows)
     exchange = {}
-    for mask in far_first(row_size):
-        lanes = pl.ds(pl.multiple_of(flip(z, mask) * piece, TILE), piece)
-        exchange[mask] = remote(coefs_ref.at[:, :, lanes], xall.at[:, own_rows, :], x_send, x_recv, mask, "row")
-        exchange[mask].start()
+    for q in range(chunks):
+        here = pl.ds(q * TILE, TILE)
+        for mask in far_first(row_size):
+            lanes = pl.ds(pl.multiple_of(flip(z, mask) * piece + q * TILE, TILE), TILE)
+            slot = q * (row_size - 1) + mask - 1
+            exchange[q, mask] = pltpu.make_async_remote_copy(
+                src_ref=coefs_ref.at[:, :, lanes], dst_ref=xall.at[:, own_rows, here],
+                send_sem=x_send.at[slot], recv_sem=x_recv.at[slot],
+                device_id={"row": flip(z, mask)}, device_id_type=MESH,
+            )
+            exchange[q, mask].start()
     own = pltpu.make_async_copy(
         coefs_ref.at[:, :, pl.ds(pl.multiple_of(z * piece, TILE), piece)], xall.at[:, own_rows, :], own_sem
     )
     own.start()
-    start_rows = pl.ds(pl.multiple_of(c * basis_rows, 8), basis_rows)
-    start[start_rows, :] = basis_ref[...]
+    start[c] = basis_ref[...]
     starts = []
     for mask in range(1, col_size):
-        copy = remote(basis_ref, start.at[start_rows, :], v_send, v_recv, mask, "col")
+        copy = remote(basis_ref, start.at[c], v_send, v_recv, mask, "col")
         copy.start()
         starts.append(copy)
 
-    wave = c * width + z * piece + lax.broadcasted_iota(jnp.int32, (1, piece), 1)
-    wave_x = jnp.abs(wave // (GRID * (GRID // 2)) - GRID // 2)
-    wave_z = wave % GRID - GRID // 2
-
-    def prepare(index):
+    wave = c * width + z * piece + lax.broadcasted_iota(jnp.int32, (TILE, TILE), 1)
+    wave_x = jnp.abs(wave // (GRID * (GRID // 2)) - GRID // 2).astype(jnp.float32)
+    wave_z = (wave % GRID - GRID // 2).astype(jnp.float32) * 16.0
+    for i in range(0, total, TILE):
+        limits = tilts_ref[:, i : i + TILE].astype(jnp.float32)
+        below = jnp.broadcast_to(limits[0:1, :], (TILE, TILE)).T
+        above = jnp.broadcast_to(limits[1:2, :], (TILE, TILE)).T
+        inside = jnp.where(wave_z >= 0, wave_z - above * wave_x, -wave_z - below * wave_x) <= 0
+        mask = jnp.where(inside, 1.0, 0.0)
+        keep[i : i + TILE, :] = mask
+        mb[i : i + TILE, :] = mask.astype(jnp.bfloat16)
+
+    for copy in starts:
+        copy.wait()
+    places = lax.broadcasted_iota(jnp.int32, (basis_rows, total), 1) - lax.broadcasted_iota(
+        jnp.int32, (basis_rows, total), 0
+    )
+    for k in range(col_size):
+        term = nn(start[k], jnp.where(places == k * basis_rows, 1.0, 0.0).astype(jnp.float32), HIGH)
+        first[...] = term if k == 0 else first[...] + term
+
+    def prepare(q, index):
         span = pl.ds(pl.multiple_of(index * rows, 16), rows)
-        tilt = tilts_ref[span, :]
-        upward = wave_z * 16 <= tilt[:, 1:2] * wave_x
-        downward = -wave_z * 16 <= tilt[:, 0:1] * wave_x
-        mask = jnp.where(jnp.logical_or(jnp.logical_and(wave_z >= 0, upward), jnp.logical_and(wave_z < 0, downward)), 1.0, 0.0)
-        mb[span, :] = mask.astype(jnp.bfloat16)
-        real = xall[0, span, :] * mask
-        imag = xall[1, span, :] * mask
-        xh[span, :piece], xl[span, :piece] = split(real)
-        xh[span, piece:], xl[span, piece:] = split(imag)
-        eh[span, :], el[span, :] = split(real * real + imag * imag)
+        lanes = slice(q * TILE, (q + 1) * TILE)
+        mask = keep[span, :]
+        real = xall[0, span, lanes] * mask
+        imag = xall[1, span, lanes] * mask
+        for part_lanes, value in ((slice(2 * q * TILE, (2 * q + 1) * TILE), real), (slice((2 * q + 1) * TILE, (2 * q + 2) * TILE), imag)):
+            xh[span, part_lanes], xl[span, part_lanes] = split(value)
+        power = real * real + imag * imag
+        if q > 0:
+            power = power + energy[span, :]
+        if q < chunks - 1:
+            energy[span, :] = power
+        else:
+            eh[span, :], el[span, :] = split(power)
+
+    def products(q):
+        lanes = slice(2 * q * TILE, 2 * (q + 1) * TILE)
+        for a in range(BLOCKS):
+            for t in range(2):
+                b = (a + t) % BLOCKS
+                right = slice(b * size, (b + 1) * size)
+                out = slice(t * size, (t + 1) * size)
+
+                def tile(index, carry, a=a, right=right, out=out):
+                    left = pl.ds(pl.multiple_of(a * size + index * TILE, TILE), TILE)
+                    value = (
+                        nt(xh[left, lanes], xh[right, lanes])
+                        + nt(xh[left, lanes], xl[right, lanes])
+                        + nt(xl[left, lanes], xh[right, lanes])
+                    )
+                    part[0, left, out] = value if q == 0 else part[0, left, out] + value
+                    if q == chunks - 1:
+                        part[1, left, out] = nt(eh[left, :], mb[right, :]) + nt(el[left, :], mb[right, :])
+                        part[2, left, out] = nt(mb[left, :], eh[right, :]) + nt(mb[left, :], el[right, :])
+                    return carry
+
+                lax.fori_loop(0, size // TILE, tile, 0)
 
     own.wait()
-    prepare(z)
-    for mask in reversed(far_first(row_size)):
-        exchange[mask].wait()
-        prepare(flip(z, mask))
-
-    for a in range(BLOCKS):
-        for t in range(2):
-            b = (a + t) % BLOCKS
-            right = slice(b * size, (b + 1) * size)
-            lanes = slice(t * size, (t + 1) * size)
-
-            def tile(index, carry, a=a, right=right, lanes=lanes):
-                left = pl.ds(pl.multiple_of(a * size + index * TILE, TILE), TILE)
-                part[0, left, lanes] = (
-                    nt(xh[left, :], xh[right, :]) + nt(xh[left, :], xl[right, :]) + nt(xl[left, :], xh[right, :])
-                )
-                part[1, left, lanes] = nt(eh[left, :], mb[right, :]) + nt(el[left, :], mb[right, :])
-                part[2, left, lanes] = nt(mb[left, :], eh[right, :]) + nt(mb[left, :], el[right, :])
-                return carry
-
-            lax.fori_loop(0, size // TILE, tile, 0)
+    for q in range(chunks):
+        prepare(q, z)
+        for mask in far_first(row_size):
+            exchange[q, mask].wait()
+            prepare(q, flip(z, mask))
+        products(q)
 
     pairs = col_size // 2
     side = c % 2
@@ -253,25 +288,19 @@
     chosen = lax.broadcasted_iota(jnp.int32, (basis_rows, total), 1)
     chosen = chosen == c * basis_rows + lax.broadcasted_iota(jnp.int32, (basis_rows, total), 0)
     chosen = jnp.where(chosen, 1.0, 0.0).astype(jnp.float32)
-    ccc_ref[...] = nt(part[0, own_rows, :], chosen[:, : 2 * size], HIGH) + nt(
-        part[1, own_rows, :size], chosen[:, 2 * size :], HIGH
-    )
-
-    for copy in starts:
-        copy.wait()
-    eig = basis_ref.shape[1]
-    unit = lax.broadcasted_iota(jnp.int32, (eig, eig), 0) == lax.broadcasted_iota(jnp.int32, (eig, eig), 1)
-    first = nt(jnp.where(unit, 1.0, 0.0).astype(jnp.float32), start[...], HIGH)
+    ccc_ref[...] = nt(chosen[:, : 2 * size], part[0, own_rows, :], HIGH) + nt(
+        chosen[:, 2 * size :], part[1, own_rows, :size], HIGH
+    )
 
     def iterate(step, current):
         high, low = split(current)
         wide = nn(high, ch[...]) + nn(high, cl[...]) + nn(low, ch[...])
         return nn_six(inverse_factor(nt(wide, wide, HIGH)), wide)
 
-    last = first
+    last = first[...]
     for step in range(ITERS):
         last = iterate(step, last)
-    out_ref[...] = nt(chosen, last, HIGH) * math.sqrt(total)
+    out_ref[...] = nt(last, chosen, HIGH) * math.sqrt(total)
 
 
 def local(coefs, tilts, start_basis):
@@ -290,19 +319,22 @@
     ccc, basis = pl.pallas_call(
         functools.partial(kernel, row_size, col_size),
         out_shape=(
-            jax.ShapeDtypeStruct((rows, basis_rows), f32),
-            jax.ShapeDtypeStruct((basis_rows, eig), f32),
+            jax.ShapeDtypeStruct((basis_rows, rows), f32),
+            jax.ShapeDtypeStruct((eig, basis_rows), f32),
         ),
         in_specs=[pl.BlockSpec(memory_space=pl.ANY), vmem, vmem],
         out_specs=(vmem, vmem),
         scratch_shapes=[
             pltpu.VMEM((2, total, piece), f32),
-            pltpu.VMEM((total, eig), f32),
+            pltpu.VMEM((col_size, eig, basis_rows), f32),
+            pltpu.VMEM((eig, total), f32),
+            pltpu.VMEM((total, TILE), f32),
+            pltpu.VMEM((total, TILE), f32),
             pltpu.VMEM((total, 2 * piece), b16),
             pltpu.VMEM((total, 2 * piece), b16),
-            pltpu.VMEM((total, piece), b16),
-            pltpu.VMEM((total, piece), b16),
-            pltpu.VMEM((total, piece), b16),
+            pltpu.VMEM((total, TILE), b16),
+            pltpu.VMEM((total, TILE), b16),
+            pltpu.VMEM((total, TILE), b16),
             pltpu.VMEM((3, total, lanes), f32),
             pltpu.VMEM((3, total // 2, lanes), f32),
             pltpu.VMEM((pairs - 1, 3, strip, lanes), f32),
@@ -311,7 +343,7 @@
             pltpu.VMEM((total, total), b16),
             pltpu.VMEM((total, total), b16),
             pltpu.SemaphoreType.DMA,
-            dma(row_size - 1), dma(row_size - 1),
+            dma(piece // TILE * (row_size - 1)), dma(piece // TILE * (row_size - 1)),
             dma(col_size - 1), dma(col_size - 1),
             dma(1), dma(1),
             dma(pairs - 1), dma(pairs - 1),
@@ -323,8 +355,8 @@
             collective_id=0, has_side_effects=True, vmem_limit_bytes=67043328
         ),
         name="subspace",
-    )(coefs, tilts, start_basis)
-    return ccc, basis
+    )(coefs, tilts.T, start_basis.T)
+    return ccc.T, basis.T
 
 
 def solution(mesh):

time: 88 us -> 84.4 us (0.959)
  local copies, waits for them, and re-layouts: 5.8 us -> 2.67 us
    pallas_call x2 -> x0, local copies, waits for them, and re-layouts: 2.9 us -> none  [local(): pl.pallas_call(functools.partial(kernel, row_size, col_size), out_shape=(...]
where the time goes in v2:
time: 84.4 us; the launch traced here: 84 us
  Pallas kernels  80.7 us (96%)
  local copies, waits for them, and re-layouts  2.67 us (3%)
    pallas_call x1, Pallas kernels, local(): pl.pallas_call(functools.partial(kernel, row_size, col_size), out_shape=(...  80.7 us
    unnamed x2, local copies, waits for them, and re-layouts  2.67 us

profile of v2, /device:TPU:0, one launch (start us, length us, event | category | flops | bytes accessed | tf_op | source)
XLA Modules:
  0.0 84.0 jit_solution(290977270330559947)
XLA Ops:
  0.6 80.7 %subspace.1 = (f32[48,96]{1,0:T(8,128)}, f32[32,48]{1,0:T(8,128)}) custom-call(f32[2,96,2048]{2,1,0:T(8,128)} %coefs_ref.1, s32[2,384]{1,0:T(2,128)} %bitcast.7, f32[32,48]{1,0:T(8,128)} %bitcast.5), custom_call_target="tpu_custom_call" | custom-call | tf_op jit(solution)/shard_map/subspace/pallas_call | solution.py:319
  81.4 1.3 %copy.7 = f32[96,48]{0,1:T(8,128)} copy(f32[96,48]{0,1:T(8,128)} %bitcast.4) | data formatting | bytes 36864
  82.7 1.3 %copy.8 = f32[48,32]{0,1:T(8,128)} copy(f32[48,32]{0,1:T(8,128)} %bitcast.6) | data formatting | bytes 12288

commit v3 on v2

--- a/solution.py
+++ b/solution.py
@@ -15,6 +15,7 @@
 MESH = pl.DeviceIdType.MESH
 TILE = 128
 BLOCKS = 3
+GROUP = 8
 
 
 def flip(index, mask):
@@ -70,15 +71,26 @@
     work = gram
     inverse = jnp.where(rows == cols, 1.0, 0.0).astype(jnp.float32)
     pivots = jnp.ones((n, n), jnp.float32)
-    for j in range(n):
-        column = jnp.broadcast_to(work[:, j : j + 1], (n, n))
-        pivot = column[j : j + 1, :]
-        reciprocal = 1.0 / pivot
-        pivots = jnp.where(rows == j, pivot, pivots)
-        factor = jnp.where(rows > j, column, 0.0)
-        inverse = inverse - factor * (inverse[j : j + 1, :] * reciprocal)
-        if j < n - 1:
-            work = work - factor * (work[j : j + 1, :] * reciprocal)
+    for j in range(0, n, GROUP):
+        columns = [jnp.broadcast_to(work[:, j + p : j + p + 1], (n, n)) for p in range(GROUP)]
+        lines = [work[j + p : j + p + 1, :] for p in range(GROUP)]
+        others = [inverse[j + p : j + p + 1, :] for p in range(GROUP)]
+        for p in range(GROUP):
+            pivot = columns[p][j + p : j + p + 1, :]
+            reciprocal = 1.0 / pivot
+            pivots = jnp.where(rows == j + p, pivot, pivots)
+            for q in range(p + 1, GROUP):
+                weight = columns[p][j + q : j + q + 1, :] * reciprocal
+                columns[q] = columns[q] - columns[p] * weight
+                lines[q] = lines[q] - lines[p] * weight
+                others[q] = others[q] - others[p] * weight
+            lines[p] = lines[p] * reciprocal
+            others[p] = others[p] * reciprocal
+            columns[p] = jnp.where(rows > j + p, columns[p], 0.0)
+        for p in range(GROUP):
+            inverse = inverse - columns[p] * others[p]
+            if j + GROUP < n:
+                work = work - columns[p] * lines[p]
     return inverse / jnp.sqrt(pivots)
 
 

time: 84.4 us -> 76.7 us (0.909)
  Pallas kernels: 80.7 us -> 73 us
    pallas_call x1, Pallas kernels: 80.7 us -> 73 us  [local(): pl.pallas_call(functools.partial(kernel, row_size, col_size), out_shape=(...]
where the time goes in v3:
time: 76.7 us; the launch traced here: 76.3 us
  Pallas kernels  73 us (95%)
  local copies, waits for them, and re-layouts  2.67 us (3%)
    pallas_call x1, Pallas kernels, local(): pl.pallas_call(functools.partial(kernel, row_size, col_size), out_shape=(...  73 us
    unnamed x2, local copies, waits for them, and re-layouts  2.67 us

profile of v3, /device:TPU:0, one launch (start us, length us, event | category | flops | bytes accessed | tf_op | source)
XLA Modules:
  0.0 76.3 jit_solution(16382668659034685961)
XLA Ops:
  0.6 73.0 %subspace.1 = (f32[48,96]{1,0:T(8,128)}, f32[32,48]{1,0:T(8,128)}) custom-call(f32[2,96,2048]{2,1,0:T(8,128)} %coefs_ref.1, s32[2,384]{1,0:T(2,128)} %bitcast.7, f32[32,48]{1,0:T(8,128)} %bitcast.5), custom_call_target="tpu_custom_call" | custom-call | tf_op jit(solution)/shard_map/subspace/pallas_call | solution.py:331
  73.6 1.3 %copy.7 = f32[96,48]{0,1:T(8,128)} copy(f32[96,48]{0,1:T(8,128)} %bitcast.4) | data formatting | bytes 36864
  75.0 1.3 %copy.8 = f32[48,32]{0,1:T(8,128)} copy(f32[48,32]{0,1:T(8,128)} %bitcast.6) | data formatting | bytes 12288

commit v4 on v3

--- a/solution.py
+++ b/solution.py
@@ -185,8 +185,7 @@
         else:
             eh[span, :], el[span, :] = split(power)
 
-    def products(q):
-        lanes = slice(2 * q * TILE, 2 * (q + 1) * TILE)
+    def blocks(write):
         for a in range(BLOCKS):
             for t in range(2):
                 b = (a + t) % BLOCKS
@@ -194,19 +193,48 @@
                 out = slice(t * size, (t + 1) * size)
 
                 def tile(index, carry, a=a, right=right, out=out):
-                    left = pl.ds(pl.multiple_of(a * size + index * TILE, TILE), TILE)
-                    value = (
-                        nt(xh[left, lanes], xh[right, lanes])
-                        + nt(xh[left, lanes], xl[right, lanes])
-                        + nt(xl[left, lanes], xh[right, lanes])
-                    )
-                    part[0, left, out] = value if q == 0 else part[0, left, out] + value
-                    if q == chunks - 1:
-                        part[1, left, out] = nt(eh[left, :], mb[right, :]) + nt(el[left, :], mb[right, :])
-                        part[2, left, out] = nt(mb[left, :], eh[right, :]) + nt(mb[left, :], el[right, :])
+                    write(pl.ds(pl.multiple_of(a * size + index * TILE, TILE), TILE), right, out)
                     return carry
 
                 lax.fori_loop(0, size // TILE, tile, 0)
+
+    def intersections(left, right, out):
+        part[1, left, out] = nt(eh[left, :], mb[right, :]) + nt(el[left, :], mb[right, :])
+        part[2, left, out] = nt(mb[left, :], eh[right, :]) + nt(mb[left, :], el[right, :])
+
+    def numerators(q, left, right, out):
+        lanes = slice(2 * q * TILE, 2 * (q + 1) * TILE)
+        value = (
+            nt(xh[left, lanes], xh[right, lanes])
+            + nt(xh[left, lanes], xl[right, lanes])
+            + nt(xl[left, lanes], xh[right, lanes])
+        )
+        part[0, left, out] = value if q == 0 else part[0, left, out] + value
+
+    pairs = col_size // 2
+    side = c % 2
+    half = total // 2
+    strip = total // col_size
+    group = c // 2
+    theirs = pl.ds(pl.multiple_of((1 - side) * half, 8), half)
+    mine = pl.ds(pl.multiple_of(side * half, 8), half)
+    planes = (slice(1, 3), slice(0, 1))
+
+    def pair_copy(turn):
+        return pltpu.make_async_remote_copy(
+            src_ref=part.at[planes[turn], theirs, :], dst_ref=rx_pair.at[planes[turn]],
+            send_sem=pair_send.at[turn], recv_sem=pair_recv.at[turn],
+            device_id={"col": flip(c, 1)}, device_id_type=MESH,
+        )
+
+    def plane_copy(turn, mask):
+        there = pl.ds(pl.multiple_of(side * half + flip(group, mask) * strip, 8), strip)
+        slot = turn * (pairs - 1) + mask - 1
+        return pltpu.make_async_remote_copy(
+            src_ref=part.at[planes[turn], there, :], dst_ref=rx_plane.at[mask - 1, planes[turn]],
+            send_sem=plane_send.at[slot], recv_sem=plane_recv.at[slot],
+            device_id={"col": flip(c, 2 * mask)}, device_id_type=MESH,
+        )
 
     own.wait()
     for q in range(chunks):
@@ -214,31 +242,23 @@
         for mask in far_first(row_size):
             exchange[q, mask].wait()
             prepare(q, flip(z, mask))
-        products(q)
-
-    pairs = col_size // 2
-    side = c % 2
-    half = total // 2
-    strip = total // col_size
-    theirs = pl.ds(pl.multiple_of((1 - side) * half, 8), half)
-    mine = pl.ds(pl.multiple_of(side * half, 8), half)
-    pair = remote(part.at[:, theirs, :], rx_pair, pair_send, pair_recv, 1, "col")
-    pair.start()
-    pair.wait()
-    part[:, mine, :] = part[:, mine, :] + rx_pair[...]
-    group = c // 2
+        if q < chunks - 1:
+            blocks(functools.partial(numerators, q))
+    blocks(intersections)
+    pair = [pair_copy(turn) for turn in range(2)]
+    pair[0].start()
+    blocks(functools.partial(numerators, chunks - 1))
+    pair[1].start()
     copies = []
-    for mask in far_first(pairs):
-        there = pl.ds(pl.multiple_of(side * half + flip(group, mask) * strip, 8), strip)
-        copy = pltpu.make_async_remote_copy(
-            src_ref=part.at[:, there, :], dst_ref=rx_plane.at[mask - 1],
-            send_sem=plane_send.at[mask - 1], recv_sem=plane_recv.at[mask - 1],
-            device_id={"col": flip(c, 2 * mask)}, device_id_type=MESH,
-        )
-        copy.start()
-        copies.append(copy)
+    for turn in range(2):
+        pair[turn].wait()
+        part[planes[turn], mine, :] = part[planes[turn], mine, :] + rx_pair[planes[turn]]
+        for mask in far_first(pairs):
+            copies.append(plane_copy(turn, mask))
+            copies[-1].start()
     for copy in copies:
         copy.wait()
+
     base = side * half + group * strip
     strip_rows = pl.ds(pl.multiple_of(base, 8), strip)
     part[:, strip_rows, :] = part[:, strip_rows, :] + sum(rx_plane[k] for k in range(pairs - 1))
@@ -357,8 +377,8 @@
             pltpu.SemaphoreType.DMA,
             dma(piece // TILE * (row_size - 1)), dma(piece // TILE * (row_size - 1)),
             dma(col_size - 1), dma(col_size - 1),
-            dma(1), dma(1),
-            dma(pairs - 1), dma(pairs - 1),
+            dma(2), dma(2),
+            dma(2 * (pairs - 1)), dma(2 * (pairs - 1)),
             dma(row_size - 1), dma(row_size - 1),
             dma(row_size - 1), dma(row_size - 1),
             dma(col_size - 1), dma(col_size - 1),

time: 76.7 us -> 75.8 us (0.988)
  Pallas kernels: 73 us -> 72.1 us
    pallas_call x1, Pallas kernels: 73 us -> 72.1 us  [local(): pl.pallas_call(functools.partial(kernel, row_size, col_size), out_shape=(...]
where the time goes in v4:
time: 75.8 us; the launch traced here: 75.4 us
  Pallas kernels  72.1 us (95%)
  local copies, waits for them, and re-layouts  2.67 us (4%)
    pallas_call x1, Pallas kernels, local(): pl.pallas_call(functools.partial(kernel, row_size, col_size), out_shape=(...  72.1 us
    unnamed x2, local copies, waits for them, and re-layouts  2.67 us

profile of v4, /device:TPU:0, one launch (start us, length us, event | category | flops | bytes accessed | tf_op | source)
XLA Modules:
  0.0 75.4 jit_solution(8326608575213050910)
XLA Ops:
  0.6 72.1 %subspace.1 = (f32[48,96]{1,0:T(8,128)}, f32[32,48]{1,0:T(8,128)}) custom-call(f32[2,96,2048]{2,1,0:T(8,128)} %coefs_ref.1, s32[2,384]{1,0:T(2,128)} %bitcast.7, f32[32,48]{1,0:T(8,128)} %bitcast.5), custom_call_target="tpu_custom_call" | custom-call | tf_op jit(solution)/shard_map/subspace/pallas_call | solution.py:351
  72.7 1.3 %copy.7 = f32[96,48]{0,1:T(8,128)} copy(f32[96,48]{0,1:T(8,128)} %bitcast.4) | data formatting | bytes 36864
  74.1 1.3 %copy.8 = f32[48,32]{0,1:T(8,128)} copy(f32[48,32]{0,1:T(8,128)} %bitcast.6) | data formatting | bytes 12288
